TPU v7x, 32 devices: a whole 2x2x4 slice. The times are simulated.
32 devices in a mesh: row: 4 (over x, core), col: 8 (over z, y).
Axes of the slice: x: 2, y: 2, z: 4, core: 2. Of those that a mesh axis runs over, the one named last changes fastest.
Arguments:
- tensor: float32 [1024, 128, 1024], P('row', 'col'), may hold values from -6 to 6
- start_basis: float32 [1024, 256], P(('row', 'col')), may hold values from -6 to 6
Outputs:
- scaled_basis: float32 [1024, 256], P(('row', 'col'))
- core: float32 [1024, 128, 256], P('row', 'col')
All inputs are finite; a program needn't handle non-finite values.
Results may differ from a plain program's by a relative error of at most 0.0003.
Values sent between devices are 32-bit elements; how exact they have to be, the bound alone decides.
A program may use at most 128 MiB of HBM per device.

v0:
```python
import functools
import math

import jax
import jax.numpy as jnp
from jax import lax
from jax.experimental import pallas as pl
from jax.experimental.pallas import tpu as pltpu
from jax.sharding import PartitionSpec as P

PASSES = 2
TILE = 256
PANEL = 32
HIGHEST = lax.Precision.HIGHEST


def split(x):
    high = x.astype(jnp.bfloat16)
    return high, (x - high.astype(jnp.float32)).astype(jnp.bfloat16)


def dot0(a, b):
    return lax.dot_general(a, b, (((0,), (0,)), ((), ())), preferred_element_type=jnp.float32)


def exact(a, b, dims):
    return lax.dot_general(a, b, (dims, ((), ())), precision=HIGHEST, preferred_element_type=jnp.float32)


def gram_kernel(x_ref, out_ref):
    @pl.when(pl.program_id(0) == 0)
    def _():
        out_ref[...] = jnp.zeros_like(out_ref)

    high, low = split(x_ref[...])
    order = x_ref.shape[1]
    at = 0
    for start in range(0, order, TILE):
        own_high, own_low = high[:, start : start + TILE], low[:, start : start + TILE]
        rest_high, rest_low = high[:, start:], low[:, start:]
        part = dot0(own_high, rest_high) + dot0(own_high, rest_low) + dot0(own_low, rest_high)
        out_ref[:, at : at + order - start] += part
        at += order - start


def packed_gram(slab):
    rows, order = slab.shape
    width = sum(order - start for start in range(0, order, TILE))
    chunk = 512
    return pl.pallas_call(
        gram_kernel,
        grid=(rows // chunk,),
        in_specs=[pl.BlockSpec((chunk, order), lambda i: (i, 0))],
        out_specs=pl.BlockSpec((TILE, width), lambda i: (0, 0)),
        out_shape=jax.ShapeDtypeStruct((TILE, width), jnp.float32),
        compiler_params=pltpu.CompilerParams(dimension_semantics=("arbitrary",)),
        name="packed_gram",
    )(slab)


def factor(gram_ref, done_ref):
    count = gram_ref.shape[0]
    sub = lax.broadcasted_iota(jnp.int32, (8, 128), 0)
    lanes = count // 128
    for c0 in range(0, count, PANEL):
        rows = lax.broadcasted_iota(jnp.int32, (PANEL, count), 0)
        cols = lax.broadcasted_iota(jnp.int32, (PANEL, count), 1)
        unit = jnp.where(cols == rows + c0, 1.0, 0.0).astype(jnp.float32)
        panel = jnp.concatenate([gram_ref[c0 : c0 + PANEL, :], unit], axis=1)
        if c0:
            panel = panel - exact(done_ref[:c0, c0 : c0 + PANEL], done_ref[:c0, :], ((0,), (0,)))
        groups = PANEL // 8
        x = [
            [panel[8 * g : 8 * g + 8, 128 * v : 128 * v + 128] for v in range(2 * lanes)]
            for g in range(groups)
        ]
        for t in range(groups):
            col = {}
            for g in range(t, groups):
                for k in range(8):
                    at = c0 + 8 * t + k
                    col[g, k] = jnp.broadcast_to(x[g][at // 128][:, at % 128 : at % 128 + 1], (8, 128))
            pivots = jnp.ones((8, 128), jnp.float32)
            for k in range(8):
                pivot = jnp.broadcast_to(col[t, k][k : k + 1, :], (8, 128))
                pivots = jnp.where(sub == k, pivot, pivots)
                if k == 7 and t == groups - 1:
                    continue
                inverse = 1.0 / pivot
                heads = {j: jnp.broadcast_to(col[t, j][k : k + 1, :], (8, 128)) for j in range(k + 1, 8)}
                tops = [jnp.broadcast_to(x[t][v][k : k + 1, :], (8, 128)) for v in range(2 * lanes)]
                for g in range(t, groups):
                    scale = col[g, k] * inverse
                    if g == t:
                        scale = jnp.where(sub > k, scale, 0.0)
                    for j in range(k + 1, 8):
                        col[g, j] = col[g, j] - scale * heads[j]
                    for v in range(2 * lanes):
                        x[g][v] = x[g][v] - scale * tops[v]
            root = 1.0 / jnp.sqrt(pivots)
            for v in range(2 * lanes):
                done_ref[c0 + 8 * t : c0 + 8 * t + 8, 128 * v : 128 * v + 128] = x[t][v] * root


def subspace_kernel(packed_ref, start_ref, out_ref, whole, tall, gram, done):
    order = start_ref.shape[0]
    at = 0
    for start in range(0, order, TILE):
        for other in range(start, order, TILE):
            block = packed_ref[:, at : at + TILE]
            whole[start : start + TILE, other : other + TILE] = block
            if other > start:
                whole[other : other + TILE, start : start + TILE] = block.T
            at += TILE
    out_ref[...] = start_ref[...]

    def step(_, carry):
        tall[...] = exact(whole[...], out_ref[...], ((1,), (0,)))
        gram[...] = exact(tall[...], tall[...], ((0,), (0,)))
        factor(gram, done)
        out_ref[...] = exact(tall[...], done[:, gram.shape[0] :], ((1,), (1,)))
        return carry

    lax.fori_loop(0, PASSES, step, 0)


def iterate(packed, start):
    order, count = start.shape
    return pl.pallas_call(
        subspace_kernel,
        in_specs=[pl.BlockSpec(memory_space=pltpu.VMEM)] * 2,
        out_specs=pl.BlockSpec(memory_space=pltpu.VMEM),
        out_shape=jax.ShapeDtypeStruct((order, count), jnp.float32),
        scratch_shapes=[
            pltpu.VMEM((order, order), jnp.float32),
            pltpu.VMEM((order, count), jnp.float32),
            pltpu.VMEM((count, count), jnp.float32),
            pltpu.VMEM((count, 2 * count), jnp.float32),
        ],
        name="iterate",
    )(packed, start)


def core_kernel(x_ref, basis_ref, out_ref):
    high, low = split(x_ref[...])
    basis_high, basis_low = split(basis_ref[...])
    dot = functools.partial(jnp.dot, preferred_element_type=jnp.float32)
    out_ref[...] = dot(high, basis_high) + dot(high, basis_low) + dot(low, basis_high)


def core_of(slab, basis):
    rows, order = slab.shape
    count = basis.shape[1]
    chunk = 512
    return pl.pallas_call(
        core_kernel,
        grid=(rows // chunk,),
        in_specs=[
            pl.BlockSpec((chunk, order), lambda i: (i, 0)),
            pl.BlockSpec((order, count), lambda i: (0, 0)),
        ],
        out_specs=pl.BlockSpec((chunk, count), lambda i: (i, 0)),
        out_shape=jax.ShapeDtypeStruct((rows, count), jnp.float32),
        compiler_params=pltpu.CompilerParams(dimension_semantics=("arbitrary",)),
        name="core",
    )(slab, basis)


def body(tensor, start_basis):
    own_count = start_basis.shape[0]
    device_slot = lax.axis_index("row") * lax.axis_size("col") + lax.axis_index("col")
    start = lax.all_gather(start_basis, ("row", "col"), axis=0, tiled=True)
    slab = tensor.reshape(-1, tensor.shape[-1])
    packed = lax.psum(packed_gram(slab), ("row", "col"))
    subspace = iterate(packed, start)
    own_slice = lax.dynamic_slice_in_dim(subspace, device_slot * own_count, own_count, 0)
    scaled_rows = math.sqrt(subspace.shape[0]) * own_slice
    core_block = core_of(slab, subspace)
    return (scaled_rows, core_block.reshape(*tensor.shape[:2], -1))


def solution(mesh):
    return jax.shard_map(
        body,
        mesh=mesh,
        in_specs=(P("row", "col", None), P(("row", "col"), None)),
        out_specs=(P(("row", "col"), None), P("row", "col", None)),
        check_vma=False,
    )
```

profile of v0, /device:TPU:0, one launch (start us, length us, event | category | flops | bytes accessed | tf_op | source)
XLA Modules:
  0.0 284.2 jit_solution(16496973244629966464)
XLA Ops:
  7.2 0.0 all-reduce.2.cloned.1.call-start
  7.2 21.3 %packed_gram.1 = f32[256,2560]{1,0:T(8,128)} custom-call(f32[4096,1024]{1,0:T(8,128)} %bitcast.2), custom_call_target="tpu_custom_call" | custom-call | tf_op jit(solution)/shard_map/packed_gram/pallas_call | solution.py:50
  28.5 0.0 all-reduce.2.cloned.1.call-update
  28.6 0.0 all-gather.2.cloned.1.call-start
  28.6 0.7 all-gather.2.cloned.1.call-update
  29.3 138.3 %all-reduce.2.cloned.1.call-done.packed_ref = f32[256,2560]{1,0:T(8,128)} async-done(((f32[256,2560]{1,0:T(8,128)}), f32[256,2560]{1,0:T(8,128)}) %all-reduce.2.cloned.1.call-update) | async-done | bytes 2621456 | tf_op jit(solution)/shard_map/psum | solution.py:174
  167.6 55.7 %all-gather.2.cloned.1.call-done.start_ref = f32[1024,256]{1,0:T(8,128)} async-done(((f32[32,256]{1,0:T(8,128)}), f32[1024,256]{1,0:T(8,128)}) %all-gather.2.cloned.1.call-update) | async-done | bytes 1048592 | tf_op jit(solution)/shard_map/all_gather | solution.py:172
  223.3 39.2 %iterate.1.basis_ref = f32[1024,256]{1,0:T(8,128)} custom-call(f32[256,2560]{1,0:T(8,128)} %all-reduce.2.cloned.1.call-done.packed_ref, f32[1024,256]{1,0:T(8,128)} %all-gather.2.cloned.1.call-done.start_ref), custom_call_target="tpu_custom_call" | custom-call | tf_op jit(solution)/shard_map/iterate/pallas_call | solution.py:129
  262.5 13.4 %core.1 = f32[4096,256]{1,0:T(8,128)} custom-call(f32[4096,1024]{1,0:T(8,128)} %bitcast.3, f32[1024,256]{1,0:T(8,128)} %iterate.1.basis_ref), custom_call_target="tpu_custom_call" | custom-call | tf_op jit(solution)/shard_map/core/pallas_call | solution.py:155
  276.0 1.4 dynamic-slice_multiply_fusion
Async XLA Ops:
  7.2 160.4 %all-reduce.2.cloned.1.call-start = ((), (), s32[]{:S(2)}) async-start(), calls=%async_computation | async-start | bytes 5242880 | tf_op jit(solution)/shard_map/psum | solution.py:174
  28.6 194.7 %all-gather.2.cloned.1.call-start = ((), (), s32[]{:S(2)}) async-start(), calls=%async_computation.1 | async-start | bytes 1081344 | tf_op jit(solution)/shard_map/all_gather | solution.py:172
Sparse Core Ops, SparseCore 0:
  28.7 138.8 all-reduce.1
  170.7 52.5 all-gather.1
where the time goes:
time: 285 us; the launch traced here: 284 us
  waiting for transfers between devices  195 us (68%)
  Pallas kernels  74 us (26%)
  between operations  14 us (5%)
    psum x1, waiting for transfers between devices, body(): packed = lax.psum(packed_gram(slab), ('row', 'col'))  138 us
    all_gather x1, waiting for transfers between devices, body(): start = lax.all_gather(start_basis, ('row', 'col'), axis=0, tiled=True)  55.7 us
    pallas_call x1, Pallas kernels, iterate(): pl.pallas_call(subspace_kernel, in_specs=[pl.BlockSpec(memory_space=pltpu...  39.2 us
    pallas_call x1, Pallas kernels, packed_gram(): pl.pallas_call(gram_kernel, grid=(rows // chunk,), in_specs=[pl.BlockSpec...  21.3 us
    pallas_call x1, Pallas kernels, core_of(): pl.pallas_call(core_kernel, grid=(rows // chunk,), in_specs=[pl.BlockSpec...  13.4 us
  transfers between devices with their start and end apart: 2, of which 2 were waited for; matrix products, arithmetic and copies ran while one was open for 0% of the time, Pallas kernels for 0%

commit v1 on v0

--- a/solution.py
+++ b/solution.py
@@ -169,7 +169,11 @@
 def body(tensor, start_basis):
     own_count = start_basis.shape[0]
     device_slot = lax.axis_index("row") * lax.axis_size("col") + lax.axis_index("col")
-    start = lax.all_gather(start_basis, ("row", "col"), axis=0, tiled=True)
+    half = start_basis.shape[1] // 2
+    left = lax.all_gather(start_basis[:, :half], ("row", "col"), axis=0, tiled=True)
+    right_own, left = lax.optimization_barrier((start_basis[:, half:], left))
+    right = lax.all_gather(right_own, ("row", "col"), axis=0, tiled=True)
+    start = jnp.concatenate([left, right], axis=1)
     slab = tensor.reshape(-1, tensor.shape[-1])
     packed = lax.psum(packed_gram(slab), ("row", "col"))
     subspace = iterate(packed, start)

time: 285 us -> 233 us (0.82)
  waiting for transfers between devices: 195 us -> 0.02 us
  blocking collectives: 0 us -> 142 us
    all_gather x0 -> x2, blocking collectives: none -> 142 us  [the longest x1 74.7 us: body(): lax.all_gather(start_basis[:, :half], ('row', 'col'), axis=0, tiled=True)]
    psum x1, waiting for transfers between devices: 138 us -> 0.01 us  [body(): packed = lax.psum(packed_gram(slab), ('row', 'col'))]
    all_gather x1 -> x0, waiting for transfers between devices: 55.7 us -> none  [body(): start = lax.all_gather(start_basis, ('row', 'col'), axis=0, tiled=True)]
  transfers between devices with their start and end apart: 2 -> 1, of which waited for: 2 -> 0; matrix products, arithmetic and copies ran while one was open for 0% -> 0% of each run, Pallas kernels for 0% -> 0%
where the time goes in v1:
time: 233 us
  blocking collectives  142 us (61%)
  Pallas kernels  74 us (32%)
  between operations  14.1 us (6%)
  other arithmetic  2.44 us (1%)
    all_gather x1, blocking collectives, body(): lax.all_gather(start_basis[:, :half], ('row', 'col'), axis=0, tiled=True)  74.7 us
    all_gather x1, blocking collectives, body(): right = lax.all_gather(right_own, ('row', 'col'), axis=0, tiled=True)  67.5 us
    pallas_call x1, Pallas kernels, iterate(): pl.pallas_call(subspace_kernel, in_specs=[pl.BlockSpec(memory_space=pltpu...  39.2 us
    pallas_call x1, Pallas kernels, packed_gram(): pl.pallas_call(gram_kernel, grid=(rows // chunk,), in_specs=[pl.BlockSpec...  21.3 us
    pallas_call x1, Pallas kernels, core_of(): pl.pallas_call(core_kernel, grid=(rows // chunk,), in_specs=[pl.BlockSpec...  13.4 us
  transfers between devices with their start and end apart: 1, of which 0 were waited for; matrix products, arithmetic and copies ran while one was open for 0% of the time, Pallas kernels for 0%

profile of v1, /device:TPU:0, one launch (start us, length us, event | category | flops | bytes accessed | tf_op | source)
XLA Modules:
  0.0 232.7 jit_solution(16322991677027114331)
XLA Ops:
  7.2 0.0 all-reduce.2.cloned.1.call-start
  7.2 0.0 copy-start
  7.2 21.3 %packed_gram.1 = f32[256,2560]{1,0:T(8,128)} custom-call(f32[4096,1024]{1,0:T(8,128)} %bitcast.2), custom_call_target="tpu_custom_call" | custom-call | tf_op jit(solution)/shard_map/packed_gram/pallas_call | solution.py:50
  28.6 0.0 all-reduce.2.cloned.1.call-update
  28.6 0.0 copy-done
  28.6 74.7 %all_gather.6 = f32[1024,128]{1,0:T(8,128)S(1)} all-gather(f32[32,128]{1,0:T(8,128)S(1)} %get-tuple-element.6), channel_id=1, replica_groups=mesh['row'=4,'col'=8] {'row','col'}, dimensions={0}, use_global_device_ids=true | all-gather | bytes 540672 | tf_op jit(solution)/shard_map/all_gather | solution.py:173
  103.3 67.5 %all_gather.7 = f32[1024,128]{1,0:T(8,128)S(1)} all-gather(f32[32,128]{1,0:T(8,128)S(1)} %get-tuple-element.5), channel_id=1, replica_groups=mesh['row'=4,'col'=8] {'row','col'}, dimensions={0}, use_global_device_ids=true | all-gather | bytes 540672 | tf_op jit(solution)/shard_map/all_gather | solution.py:175
  170.8 1.1 pad_maximum_fusion.start_ref
  171.8 0.0 all-reduce.2.cloned.1.call-done.packed_ref
  171.8 39.2 %iterate.1.basis_ref = f32[1024,256]{1,0:T(8,128)} custom-call(f32[256,2560]{1,0:T(8,128)} %all-reduce.2.cloned.1.call-done.packed_ref, f32[1024,256]{1,0:T(8,128)} %pad_maximum_fusion.start_ref), custom_call_target="tpu_custom_call" | custom-call | tf_op jit(solution)/shard_map/iterate/pallas_call | solution.py:129
  211.1 13.4 %core.1 = f32[4096,256]{1,0:T(8,128)} custom-call(f32[4096,1024]{1,0:T(8,128)} %bitcast.3, f32[1024,256]{1,0:T(8,128)} %iterate.1.basis_ref), custom_call_target="tpu_custom_call" | custom-call | tf_op jit(solution)/shard_map/core/pallas_call | solution.py:155
  224.5 1.4 dynamic-slice_multiply_fusion
  (1 shorter events, 0.0 us)
Async XLA Ops:
  7.2 164.7 %all-reduce.2.cloned.1.call-start = ((), (), s32[]{:S(2)}) async-start(), calls=%async_computation | async-start | bytes 5242880 | tf_op jit(solution)/shard_map/psum | solution.py:178
  7.2 21.4 %copy-start = (f32[32,256]{1,0:T(8,128)S(1)}, f32[32,256]{1,0:T(8,128)}, u32[]{:S(2)}) copy-start(f32[32,256]{1,0:T(8,128)} %param.3) | copy-start | bytes 98308
Sparse Core Ops, SparseCore 0:
  28.7 140.4 all-reduce.1
